TPU v7x, 32 devices: a whole 2x2x4 slice. The times are simulated.
32 devices in a mesh: band: 4 (over x, core), grid: 8 (over z, y).
Axes of the slice: x: 2, y: 2, z: 4, core: 2. Of those that a mesh axis runs over, the one named last changes fastest.
Arguments:
- orbitals: float32 [8, 128, 128, 128], P('band', 'grid'), may hold values from -6 to 6
- occupation: float32 [8], P('band'), may hold values from 0.25 to 1
- g_list: int32 [131072], P('grid'), may hold values from 0 to 262143, as said below
- positions: float32 [3, 512], replicated, may hold values from 0 to 1
- species: int32 [512], replicated, may hold values from 0 to 3
- widths: float32 [4], replicated, may hold values from 0.3 to 2
Outputs:
- stress: float32 [3, 3], replicated
- atom_terms: float32 [512], replicated
Inputs may be any that keep to these rules, and one draw needn't show every extreme that they name: `g_list`: within each aligned block of 16384 entries the values are distinct and increasing.
All inputs are finite; a program needn't handle non-finite values.
Results may differ from a plain program's by a relative error of at most 0.00013.
Values sent between devices are 32-bit elements; how exact they have to be, the bound alone decides.
No kernel may reach another device: no remote copies, remote signals or barrier semaphores. Data moves between devices by JAX's collectives and lax.ppermute only.
A program may use at most 64 MiB of HBM per device.

v0:
```python
import math

import jax
import jax.numpy as jnp
from jax import lax
from jax.sharding import PartitionSpec as P

HIGHEST = lax.Precision.HIGHEST


def shifted(array, axis, by):
    peers = lax.axis_size(axis)
    return lax.ppermute(array, axis, [(i, (i + by) % peers) for i in range(peers)])


def dft_tables(length):
    indices = jnp.arange(length, dtype=jnp.int32)
    products = indices[:, None] * indices[None, :] % length
    angles = 2.0 * math.pi / length * products.astype(jnp.float32)
    return (jnp.cos(angles), jnp.sin(angles))


def folded_frequency(cell, length):
    folded = jnp.where(cell < length // 2, cell, cell - length)
    return folded.astype(jnp.float32)


def spectrum_sums(
    selected, freq_x, freq_y, freq_z, positions, species, widths, lengths, band_total
):
    two_pi = 2.0 * math.pi
    wave_vector = jnp.stack(
        [two_pi * freq_x / lengths[0], two_pi * freq_y / lengths[1], two_pi * freq_z / lengths[2]]
    )
    wave_square = jnp.sum(wave_vector * wave_vector, axis=0)
    nonzero = (wave_square > 0).astype(jnp.float32)
    denominator = wave_square + 1.0 - nonzero
    weighted = selected * (4.0 * math.pi) * nonzero / denominator
    identity = jnp.eye(3, dtype=jnp.float32)[:, :, None]
    kernel = 2.0 * wave_vector[:, None, :] * wave_vector[None, :, :] / denominator - identity
    stress = jnp.sum(kernel * weighted[None, None, :], axis=2) / band_total
    form_factor = (
        jnp.exp(-0.5 * wave_square[None, :] * (widths * widths)[:, None]) * weighted[None, :]
    )
    kinds = widths.shape[0]
    one_hot = (species[:, None] == jnp.arange(kinds, dtype=jnp.int32)[None, :]).astype(jnp.float32)
    atom_count = species.shape[0]
    fractions = positions.reshape(3, atom_count // 32, 32).transpose(1, 0, 2)
    hot_rows = one_hot.reshape(atom_count // 32, 32, kinds)

    def atom_block(operands):
        fraction, hot_block = operands
        phases = two_pi * (
            fraction[0][:, None] * freq_x[None, :]
            + fraction[1][:, None] * freq_y[None, :]
            + fraction[2][:, None] * freq_z[None, :]
        )
        projected = jnp.dot(jnp.cos(phases), form_factor.T, precision=HIGHEST)
        return jnp.sum(projected * hot_block, axis=1)

    atom_terms = lax.map(atom_block, (fractions, hot_rows)).reshape(atom_count) / band_total
    return (stress, atom_terms)


def per_device(orbitals, occupation, g_list, positions, species, widths):
    block_bands, slab_x, size_y, size_z = orbitals.shape
    grid_count = lax.axis_size("grid")
    band_count = lax.axis_size("band")
    size_x = slab_x * grid_count
    slab_y = size_y // grid_count
    cells = size_x * size_y * size_z
    scale = 1.0 / (float(cells) * float(cells))
    cos_x, sin_x = dft_tables(size_x)
    cos_y, sin_y = dft_tables(size_y)
    cos_z, sin_z = dft_tables(size_z)

    def finish_x(exchanged):
        real_part = exchanged[:, 0]
        imag_part = exchanged[:, 1]
        real_x = jnp.einsum("pxyz,mx->pmyz", real_part, cos_x, precision=HIGHEST) + jnp.einsum(
            "pxyz,mx->pmyz", imag_part, sin_x, precision=HIGHEST
        )
        imag_x = jnp.einsum("pxyz,mx->pmyz", imag_part, cos_x, precision=HIGHEST) - jnp.einsum(
            "pxyz,mx->pmyz", real_part, sin_x, precision=HIGHEST
        )
        return real_x * real_x + imag_x * imag_x

    def add_pairs(accumulated, right_rows, right_occupied, factor):

        def one_band(band_index, running):
            orbital_row = lax.dynamic_index_in_dim(orbitals, band_index, 0, keepdims=False)
            occupied = lax.dynamic_index_in_dim(occupation, band_index, 0, keepdims=False)
            pair_rows = orbital_row[None] * right_rows
            weights = occupied * right_occupied * (factor * scale)
            real_z = jnp.einsum("pxyz,kz->pxyk", pair_rows, cos_z, precision=HIGHEST)
            imag_z = -jnp.einsum("pxyz,kz->pxyk", pair_rows, sin_z, precision=HIGHEST)
            real_y = jnp.einsum("pxyk,my->pxmk", real_z, cos_y, precision=HIGHEST) + jnp.einsum(
                "pxyk,my->pxmk", imag_z, sin_y, precision=HIGHEST
            )
            imag_y = jnp.einsum("pxyk,my->pxmk", imag_z, cos_y, precision=HIGHEST) - jnp.einsum(
                "pxyk,my->pxmk", real_z, sin_y, precision=HIGHEST
            )
            stacked = jnp.stack([real_y, imag_y], axis=1)
            pair_power = finish_x(
                lax.all_to_all(stacked, "grid", split_axis=3, concat_axis=2, tiled=True)
            )
            return running + jnp.einsum("p,pxyz->xyz", weights, pair_power, precision=HIGHEST)

        return lax.fori_loop(0, block_bands, one_band, accumulated)

    empty = jnp.zeros((size_x, slab_y, size_z), jnp.float32)
    spectrum = add_pairs(empty, orbitals, occupation, 1.0)
    for distance in range(1, band_count // 2 + 1):
        neighbour = shifted((orbitals, occupation), "band", distance)
        factor = 2.0 if 2 * distance < band_count else 1.0
        spectrum = add_pairs(spectrum, neighbour[0], neighbour[1], factor)
    flat_spectrum = spectrum.reshape(-1)
    selected = jnp.take(flat_spectrum, g_list)
    cell_x = g_list // (slab_y * size_z)
    cell_y = lax.axis_index("grid") * slab_y + g_list // size_z % slab_y
    cell_z = g_list % size_z
    stress, atom_terms = spectrum_sums(
        selected,
        folded_frequency(cell_x, size_x),
        folded_frequency(cell_y, size_y),
        folded_frequency(cell_z, size_z),
        positions,
        species,
        widths,
        (size_x, size_y, size_z),
        block_bands * band_count,
    )
    stress, atom_terms = lax.psum((stress, atom_terms), ("band", "grid"))
    return (stress, atom_terms)


def solution(mesh):
    return jax.shard_map(
        per_device,
        mesh=mesh,
        in_specs=(P("band", "grid", None, None), P("band"), P("grid"), P(), P(), P()),
        out_specs=(P(), P()),
        check_vma=False,
    )
```

profile of v0, /device:TPU:12, one launch (start us, length us, event | category | flops | bytes accessed | tf_op | source)
XLA Modules:
  0.0 1331.4 jit_solution(5733320906474539223)
XLA Ops:
  13.5 339.4 %while.62 = (s32[]{:T(128)}, f32[128,16,128]{2,1,0:T(8,128)S(1)}, f32[2]{0:T(128)}, f32[2,16,128,128]{3,2,1,0:T(8,128)}, s32[]{:T(128)}, /*index=5*/s32[]{:T(128)}) while((s32[]{:T(128)}, f32[128,16,128]{2,1,0:T(8,128)S(1)}, f32[2]{0:T(128)}, f32[2,16,128,128]{3,2,1,0:T(8,128)}, s32[]{:T(128)}, ...), condition=%wide.region_2.3_spmd.clone.clone, body=%wide.region_1.2_spmd.clone.clone.sunk | while | flops 8068988928 | bytes 146800944 | solution.py:109
  24.2 3.7 add_bitcast_fusion.16
  33.9 5.5 copy.157
  39.4 6.4 all-to-all-start.2
  46.4 89.6 %all-to-all-done.2 = f32[2,2,16,128,128]{4,2,0,1,3:T(8,128)} async-done(((f32[2,2,16,128,128]{4,2,0,1,3:T(8,128)}), f32[2,2,16,128,128]{4,2,0,1,3:T(8,128)}, u32[]{:S(2)}, u32[]{:S(2)}) %all-to-all-start.2) | async-done | bytes 4194336 | tf_op jit(solution)/shard_map/while/body/eval_jaxpr/all_to_all | solution.py:105
  135.9 4.6 copy.158
  162.9 8.2 fusion.552
  182.2 3.7 add_bitcast_fusion.16
  192.0 5.5 copy.157
  197.4 8.0 all-to-all-start.2
  206.0 88.7 %all-to-all-done.2 = f32[2,2,16,128,128]{4,2,0,1,3:T(8,128)} async-done(((f32[2,2,16,128,128]{4,2,0,1,3:T(8,128)}), f32[2,2,16,128,128]{4,2,0,1,3:T(8,128)}, u32[]{:S(2)}, u32[]{:S(2)}) %all-to-all-start.2) | async-done | bytes 4194336 | tf_op jit(solution)/shard_map/while/body/eval_jaxpr/all_to_all | solution.py:105
  294.7 4.6 copy.158
  321.8 8.2 fusion.552
  352.9 323.8 %while.60 = (s32[]{:T(128)}, f32[128,16,128]{2,1,0:T(8,128)S(1)}, f32[2]{0:T(128)}, f32[2]{0:T(128)}, f32[2,16,128,128]{3,2,1,0:T(8,128)}, /*index=5*/f32[2,16,128,128]{3,2,1,0:T(8,128)}, s32[]{:T(128)}) while((s32[]{:T(128)}, f32[128,16,128]{2,1,0:T(8,128)S(1)}, f32[2]{0:T(128)}, f32[2]{0:T(128)}, ...), condition=%wide.region_4.5_spmd.clone.clone, body=%wide.region_3.4_spmd.clone.clone.sunk | while | flops 8068726784 | bytes 138412304 | solution.py:109
  354.2 3.9 fusion.484
  358.1 3.7 fusion.486
  366.2 3.7 add_bitcast_fusion.12
  375.9 5.5 copy.147
  381.4 8.0 all-to-all-start
  390.0 88.6 %all-to-all-done = f32[2,2,16,128,128]{4,2,0,1,3:T(8,128)} async-done(((f32[2,2,16,128,128]{4,2,0,1,3:T(8,128)}), f32[2,2,16,128,128]{4,2,0,1,3:T(8,128)}, u32[]{:S(2)}, u32[]{:S(2)}) %all-to-all-start) | async-done | bytes 4194336 | tf_op jit(solution)/shard_map/while/body/eval_jaxpr/all_to_all | solution.py:105
  478.7 4.6 copy.148
  505.7 8.9 fusion.492
  516.1 3.9 fusion.484
  528.1 3.7 add_bitcast_fusion.12
  537.9 5.5 copy.147
  543.4 8.0 all-to-all-start
  551.9 88.6 %all-to-all-done = f32[2,2,16,128,128]{4,2,0,1,3:T(8,128)} async-done(((f32[2,2,16,128,128]{4,2,0,1,3:T(8,128)}), f32[2,2,16,128,128]{4,2,0,1,3:T(8,128)}, u32[]{:S(2)}, u32[]{:S(2)}) %all-to-all-start) | async-done | bytes 4194336 | tf_op jit(solution)/shard_map/while/body/eval_jaxpr/all_to_all | solution.py:105
  640.6 4.6 copy.148
  667.6 8.9 fusion.492
  676.8 354.2 %while.61 = (s32[]{:T(128)}, f32[128,16,128]{2,1,0:T(8,128)S(1)}, f32[2]{0:T(128)}, f32[2]{0:T(128)}, f32[2,16,128,128]{3,2,1,0:T(8,128)}, /*index=5*/f32[2,16,128,128]{3,2,1,0:T(8,128)}, s32[]{:T(128)}) while((s32[]{:T(128)}, f32[128,16,128]{2,1,0:T(8,128)S(1)}, f32[2]{0:T(128)}, f32[2]{0:T(128)}, ...), condition=%wide.region_6.7_spmd.clone.clone, body=%wide.region_5.6_spmd.clone.clone.sunk | while | flops 8068726784 | bytes 138412304 | solution.py:109
  700.6 3.9 fusion.514
  704.5 3.7 fusion.516
  712.6 3.7 add_bitcast_fusion.14
  722.3 5.5 copy.152
  727.8 8.0 all-to-all-start.1
  736.4 88.7 %all-to-all-done.1 = f32[2,2,16,128,128]{4,2,0,1,3:T(8,128)} async-done(((f32[2,2,16,128,128]{4,2,0,1,3:T(8,128)}), f32[2,2,16,128,128]{4,2,0,1,3:T(8,128)}, u32[]{:S(2)}, u32[]{:S(2)}) %all-to-all-start.1) | async-done | bytes 4194336 | tf_op jit(solution)/shard_map/while/body/eval_jaxpr/all_to_all | solution.py:105
  825.0 4.6 copy.153
  852.1 8.9 fusion.522
  862.5 3.9 fusion.514
  874.5 3.7 add_bitcast_fusion.14
  884.3 5.5 copy.152
  889.7 8.0 all-to-all-start.1
  898.3 88.7 %all-to-all-done.1 = f32[2,2,16,128,128]{4,2,0,1,3:T(8,128)} async-done(((f32[2,2,16,128,128]{4,2,0,1,3:T(8,128)}), f32[2,2,16,128,128]{4,2,0,1,3:T(8,128)}, u32[]{:S(2)}, u32[]{:S(2)}) %all-to-all-start.1) | async-done | bytes 4194336 | tf_op jit(solution)/shard_map/while/body/eval_jaxpr/all_to_all | solution.py:105
  987.0 4.6 copy.153
  1014.0 8.9 fusion.522
  1031.1 90.5 %gather_fusion = f32[16384]{0:T(1024)S(1)} fusion(f32[262144]{0:T(1024)S(1)} %bitcast.377, s32[16384]{0:T(1024)S(1)} %copy-done.11), kind=kCustom, calls=%fused_computation | custom fusion | bytes 196608 | tf_op jit(solution)/shard_map/jit(_take)/gather | solution.py:118
  1122.3 166.4 %while.59 = (s32[]{:T(128)}, f32[16,32]{1,0:T(8,128)S(1)}, f32[16,3,32]{2,0,1:T(8,128)}, f32[16384]{0:T(1024)S(1)}, f32[16384]{0:T(1024)S(1)}, /*index=5*/f32[16...) while((s32[]{:T(128)}, f32[16,32]{1,0:T(8,128)S(1)}, ...), condition=%wide.region_11.12_spmd.clone, body=%wide.region_9.11_spmd.clone.sunk | while | flops 28442852 | bytes 329921 | solution.py:61
  1123.0 9.6 fusion.462
  1133.4 9.6 fusion.462
  1143.8 9.6 fusion.462
  1154.2 9.6 fusion.462
  1164.6 9.6 fusion.462
  1175.0 9.6 fusion.462
  1185.4 9.6 fusion.462
  1195.8 9.7 fusion.462
  1206.2 9.6 fusion.462
  1216.6 9.7 fusion.462
  1227.1 9.6 fusion.462
  1237.5 9.7 fusion.462
  1247.9 9.6 fusion.462
  1258.3 9.6 fusion.462
  1268.7 9.6 fusion.462
  1279.1 9.6 fusion.462
  1288.8 42.1 %all-reduce = (f32[3,3]{1,0:T(4,128)}, f32[512]{0:T(512)}) all-reduce(f32[3,3]{1,0:T(4,128)S(1)} %broadcast_multiply_fusion.6, f32[512]{0:T(512)S(1)} %div.77), channel_id=1, replica_groups=mesh['band'=4,'grid'=8] {'band','grid'}, use_global_device_ids=true, to_apply=%region_8.9 | all-reduce | flops 521 | bytes 4168 | tf_op jit(solution)/shard_map/psum | solution.py:133
  (213 shorter events, 251.6 us)
Async XLA Ops:
  0.6 352.2 %collective-permute-start.1 = (f32[2,16,128,128]{3,2,1,0:T(8,128)}, f32[2,16,128,128]{3,2,1,0:T(8,128)}, u32[]{:S(2)}, u32[]{:S(2)}) collective-permute-start(f32[2,16,128,128]{3,2,1,0:T(8,128)} %param.14), channel_id=1, source_target_pairs={{0,8},{8,16},{16,24},{24,0},{1,9},{9,17},{17,25},{25,1},{2,10},{10... | collective-permute-start | bytes 6291464 | tf_op jit(solution)/shard_map/ppermute | solution.py:13
  0.7 676.0 %collective-permute-start.3 = (f32[2,16,128,128]{3,2,1,0:T(8,128)}, f32[2,16,128,128]{3,2,1,0:T(8,128)}, u32[]{:S(2)}, u32[]{:S(2)}) collective-permute-start(f32[2,16,128,128]{3,2,1,0:T(8,128)} %param.14), channel_id=1, source_target_pairs={{0,16},{8,24},{16,0},{24,8},{1,17},{9,25},{17,1},{25,9},{2,18},{10... | collective-permute-start | bytes 6291464 | tf_op jit(solution)/shard_map/ppermute | solution.py:13
  2.3 350.6 %collective-permute-start = (f32[2]{0:T(128)}, f32[2]{0:T(128)}, u32[]{:S(2)}, u32[]{:S(2)}) collective-permute-start(f32[2]{0:T(128)} %param.15), channel_id=1, source_target_pairs={{0,8},{8,16},{16,24},{24,0},{1,9},{9,17},{17,25},{25,1},{2,10},{10... | collective-permute-start | bytes 32 | tf_op jit(solution)/shard_map/ppermute | solution.py:13
  2.5 350.3 %collective-permute-start.2 = (f32[2]{0:T(128)}, f32[2]{0:T(128)}, u32[]{:S(2)}, u32[]{:S(2)}) collective-permute-start(f32[2]{0:T(128)} %param.15), channel_id=1, source_target_pairs={{0,16},{8,24},{16,0},{24,8},{1,17},{9,25},{17,1},{25,9},{2,18},{10... | collective-permute-start | bytes 32 | tf_op jit(solution)/shard_map/ppermute | solution.py:13
  13.5 1.9 copy-start
  39.4 6.4 copy-start.17
  39.4 96.5 %all-to-all-start.2 = ((f32[2,2,16,128,128]{4,2,0,1,3:T(8,128)}), f32[2,2,16,128,128]{4,2,0,1,3:T(8,128)}, u32[]{:S(2)}, u32[]{:S(2)}) async-start(f32[2,2,16,128,128]{4,2,0,1,3:T(8,128)} %copy.157), calls=%async_computation.2 | async-start | bytes 8388608 | tf_op jit(solution)/shard_map/while/body/eval_jaxpr/all_to_all | solution.py:105
  153.5 2.1 copy-start.1
  153.5 2.2 copy-start.2
  171.5 1.9 copy-start
  197.4 8.0 copy-start.17
  197.4 97.3 %all-to-all-start.2 = ((f32[2,2,16,128,128]{4,2,0,1,3:T(8,128)}), f32[2,2,16,128,128]{4,2,0,1,3:T(8,128)}, u32[]{:S(2)}, u32[]{:S(2)}) async-start(f32[2,2,16,128,128]{4,2,0,1,3:T(8,128)} %copy.157), calls=%async_computation.2 | async-start | bytes 8388608 | tf_op jit(solution)/shard_map/while/body/eval_jaxpr/all_to_all | solution.py:105
  312.3 2.1 copy-start.1
  312.3 2.2 copy-start.2
  381.4 8.0 copy-start.18
  381.4 97.2 %all-to-all-start = ((f32[2,2,16,128,128]{4,2,0,1,3:T(8,128)}), f32[2,2,16,128,128]{4,2,0,1,3:T(8,128)}, u32[]{:S(2)}, u32[]{:S(2)}) async-start(f32[2,2,16,128,128]{4,2,0,1,3:T(8,128)} %copy.147), calls=%async_computation | async-start | bytes 8388608 | tf_op jit(solution)/shard_map/while/body/eval_jaxpr/all_to_all | solution.py:105
  496.2 2.1 copy-start.3
  496.2 2.2 copy-start.4
  543.4 8.0 copy-start.18
  543.4 97.2 %all-to-all-start = ((f32[2,2,16,128,128]{4,2,0,1,3:T(8,128)}), f32[2,2,16,128,128]{4,2,0,1,3:T(8,128)}, u32[]{:S(2)}, u32[]{:S(2)}) async-start(f32[2,2,16,128,128]{4,2,0,1,3:T(8,128)} %copy.147), calls=%async_computation | async-start | bytes 8388608 | tf_op jit(solution)/shard_map/while/body/eval_jaxpr/all_to_all | solution.py:105
  658.1 2.1 copy-start.3
  658.1 2.2 copy-start.4
  676.7 354.3 %copy-start.11 = (s32[16384]{0:T(1024)S(1)}, s32[16384]{0:T(1024)}, u32[]{:S(2)}) copy-start(s32[16384]{0:T(1024)} %fusion.346) | copy-start | bytes 196612
  727.8 8.0 copy-start.19
  727.8 97.2 %all-to-all-start.1 = ((f32[2,2,16,128,128]{4,2,0,1,3:T(8,128)}), f32[2,2,16,128,128]{4,2,0,1,3:T(8,128)}, u32[]{:S(2)}, u32[]{:S(2)}) async-start(f32[2,2,16,128,128]{4,2,0,1,3:T(8,128)} %copy.152), calls=%async_computation.1 | async-start | bytes 8388608 | tf_op jit(solution)/shard_map/while/body/eval_jaxpr/all_to_all | solution.py:105
  842.6 2.1 copy-start.5
  842.6 2.2 copy-start.6
  889.7 8.0 copy-start.19
  889.7 97.2 %all-to-all-start.1 = ((f32[2,2,16,128,128]{4,2,0,1,3:T(8,128)}), f32[2,2,16,128,128]{4,2,0,1,3:T(8,128)}, u32[]{:S(2)}, u32[]{:S(2)}) async-start(f32[2,2,16,128,128]{4,2,0,1,3:T(8,128)} %copy.152), calls=%async_computation.1 | async-start | bytes 8388608 | tf_op jit(solution)/shard_map/while/body/eval_jaxpr/all_to_all | solution.py:105
  1004.5 2.1 copy-start.5
  1004.5 2.2 copy-start.6
  1031.0 90.7 %copy-start.9 = (s32[16384]{0:T(1024)S(1)}, s32[16384]{0:T(1024)}, u32[]{:S(2)}) copy-start(s32[16384]{0:T(1024)} %param.16) | copy-start | bytes 196612
  1031.0 90.6 %copy-start.10 = (f32[16384]{0:T(1024)S(1)}, f32[16384]{0:T(1024)}, u32[]{:S(2)}) copy-start(f32[16384]{0:T(1024)} %get-tuple-element.865) | copy-start | bytes 196612
  1031.0 90.7 %copy-start.7 = (f32[3,16384]{1,0:T(4,128)S(1)}, f32[3,16384]{1,0:T(4,128)}, u32[]{:S(2)}) copy-start(f32[3,16384]{1,0:T(4,128)} %get-tuple-element.864) | copy-start | bytes 589828
  1031.0 90.7 %copy-start.8 = (f32[3,16384]{1,0:T(4,128)S(1)}, f32[3,16384]{1,0:T(4,128)}, u32[]{:S(2)}) copy-start(f32[3,16384]{1,0:T(4,128)} %get-tuple-element.866) | copy-start | bytes 589828
  1031.1 90.7 %copy-start.15 = (f32[3,3]{1,0:T(4,128)S(1)}, f32[3,3]{1,0:T(4,128)}, u32[]{:S(2)}) copy-start(f32[3,3]{1,0:T(4,128)} %fusion.349) | copy-start | bytes 112
  1031.1 91.2 %copy-start.12 = (f32[16384]{0:T(1024)S(1)}, f32[16384]{0:T(1024)}, u32[]{:S(2)}) copy-start(f32[16384]{0:T(1024)} %get-tuple-element.1115) | copy-start | bytes 196612
  1031.1 91.2 %copy-start.13 = (f32[16384]{0:T(1024)S(1)}, f32[16384]{0:T(1024)}, u32[]{:S(2)}) copy-start(f32[16384]{0:T(1024)} %get-tuple-element.1117) | copy-start | bytes 196612
  1031.1 91.2 %copy-start.14 = (f32[16384]{0:T(1024)S(1)}, f32[16384]{0:T(1024)}, u32[]{:S(2)}) copy-start(f32[16384]{0:T(1024)} %get-tuple-element.1116) | copy-start | bytes 196612
  1031.1 91.2 %copy-start.16 = (f32[16,32]{1,0:T(8,128)S(1)}, f32[16,32]{1,0:T(8,128)}, u32[]{:S(2)}) copy-start(f32[16,32]{1,0:T(8,128)} %custom-call.3) | copy-start | bytes 6148
  1031.1 91.2 %copy-start.20 = (f32[4]{0:T(128)S(1)}, f32[4]{0:T(128)}, u32[]{:S(2)}) copy-start(f32[4]{0:T(128)} %mul.627) | copy-start | bytes 52
where the time goes:
time: 1360 us; the launch traced here: 1330 us
  waiting for transfers between devices  533 us (39%)
  matrix products  391 us (29%)
  local copies, waits for them, and re-layouts  237 us (17%)
  loops' own time  54.2 us (4%)
  starting transfers between devices  49.7 us (4%)
  blocking collectives  42.1 us (3%)
  other arithmetic  23.1 us (2%)
    all_to_all x6, waiting for transfers between devices, one_band(): lax.all_to_all(stacked, 'grid', split_axis=3, concat_axis=2, tiled=True)  533 us
    dot_general x16, matrix products, atom_block(): projected = jnp.dot(jnp.cos(phases), form_factor.T, precision=HIGHEST)  154 us
    gather x1, local copies, waits for them, and re-layouts, per_device(): selected = jnp.take(flat_spectrum, g_list)  90.5 us
    another operation x3, loops' own time, add_pairs(): return lax.fori_loop(0, block_bands, one_band, accumulated)  53.9 us
    dot_general x6, matrix products, one_band(): jnp.einsum('p,pxyz->xyz', weights, pair_power, precision=HIGHEST)  52 us
    all_to_all x6, starting transfers between devices, one_band(): lax.all_to_all(stacked, 'grid', split_axis=3, concat_axis=2, tiled=True)  46.3 us
    psum x1, blocking collectives, per_device(): stress, atom_terms = lax.psum((stress, atom_terms), ('band', 'grid'))  42.1 us
    another operation x6, local copies, waits for them, and re-layouts, one_band(): stacked = jnp.stack([real_y, imag_y], axis=1)  32.8 us
  transfers between devices with their start and end apart: 10, of which 6 were waited for; matrix products, arithmetic and copies ran while one was open for 20% of the time, Pallas kernels for 0%

commit v1 on v0

v1 whole, which is shorter than its diff:
```python
import functools
import math

import jax
import jax.numpy as jnp
from jax import lax
from jax.experimental import pallas as pl
from jax.experimental.pallas import tpu as pltpu
from jax.sharding import PartitionSpec as P

HIGH = lax.Precision.HIGH


def shifted(array, axis, by):
    peers = lax.axis_size(axis)
    return lax.ppermute(array, axis, [(i, (i + by) % peers) for i in range(peers)])


def dft_tables(length):
    indices = jnp.arange(length, dtype=jnp.int32)
    products = indices[:, None] * indices[None, :] % length
    angles = 2.0 * math.pi / length * products.astype(jnp.float32)
    return (jnp.cos(angles), jnp.sin(angles))


def folded(cell, length, nyquist_up):
    keep = cell <= length // 2 if nyquist_up else cell < length // 2
    return jnp.where(keep, cell, cell - length).astype(jnp.float32)


def mask_kernel(chunks, row_ref, col_ref, out_ref):
    step = pl.program_id(0)
    rows, cols = out_ref.shape[1:]
    width = row_ref.shape[-1]

    @pl.when((step == 0) | (step == chunks))
    def _():
        out_ref[...] = jnp.zeros_like(out_ref)

    one_row = lax.broadcasted_iota(jnp.int32, (rows, width), 0) == row_ref[0]
    one_col = lax.broadcasted_iota(jnp.int32, (cols, width), 0) == col_ref[0]
    out_ref[0] += lax.dot_general(
        one_row.astype(jnp.bfloat16),
        one_col.astype(jnp.bfloat16),
        (((1,), (1,)), ((), ())),
        preferred_element_type=jnp.float32,
    )


def entry_masks(row_ids, col_ids, rows, cols):
    entries = row_ids.shape[1]
    width = math.gcd(entries, 512)
    chunks = entries // width
    row_ids = row_ids.reshape(3 * chunks, 1, width)
    col_ids = col_ids.reshape(3 * chunks, 1, width)
    id_spec = pl.BlockSpec((1, 1, width), lambda i: (i, 0, 0))
    return pl.pallas_call(
        functools.partial(mask_kernel, chunks),
        grid=(3 * chunks,),
        in_specs=[id_spec, id_spec],
        out_specs=pl.BlockSpec((1, rows, cols), lambda i: (jnp.where(i < chunks, 0, 1), 0, 0)),
        out_shape=jax.ShapeDtypeStruct((2, rows, cols), jnp.float32),
        compiler_params=pltpu.CompilerParams(dimension_semantics=("arbitrary",)),
        cost_estimate=pl.CostEstimate(
            flops=12 * entries * rows * cols, bytes_accessed=2 * rows * cols * 4, transcendentals=0
        ),
        name="entry_masks",
    )(row_ids, col_ids)


def per_device(orbitals, occupation, g_list, positions, species, widths):
    block_bands, slab_x, size_y, size_z = orbitals.shape
    grid_count = lax.axis_size("grid")
    band_count = lax.axis_size("band")
    band_index = lax.axis_index("band")
    grid_index = lax.axis_index("grid")
    size_x = slab_x * grid_count
    slab_y = size_y // grid_count
    cells = size_x * size_y * size_z
    scale = 1.0 / float(cells)

    own = jnp.transpose(orbitals, (0, 2, 1, 3))
    others = {}
    for distance in range(1, band_count // 2 + 1):
        others[distance] = shifted((own, occupation), "band", distance)

    def split(code):
        return (
            code // (slab_y * size_z),
            code // size_z % slab_y,
            code % size_z,
        )

    mirror = lax.ppermute(
        g_list, "grid", [(d, grid_count - 1 - d) for d in range(grid_count)]
    )
    mirror_zero = lax.ppermute(
        g_list, "grid", [(d, (grid_count - d) % grid_count) for d in range(grid_count)]
    )
    own_x, own_y, own_z = split(g_list)
    mir_x, mir_y, mir_z = split(mirror)
    zer_x, zer_y, zer_z = split(mirror_zero)
    row_ids = jnp.stack(
        [
            own_y * size_x + own_x,
            jnp.where(mir_y > 0, (slab_y - mir_y) * size_x + (size_x - mir_x) % size_x, -1),
            jnp.where(zer_y == 0, (size_x - zer_x) % size_x, -1),
        ]
    )
    col_ids = jnp.stack([own_z, (size_z - mir_z) % size_z, (size_z - zer_z) % size_z])
    masks = entry_masks(row_ids, col_ids, slab_y * size_x, size_z)
    masks = masks.reshape(2, slab_y, size_x, size_z)

    cos_x, sin_x = dft_tables(size_x)
    cos_y, sin_y = dft_tables(size_y)
    cos_z, sin_z = dft_tables(size_z)
    z_real = jnp.concatenate([cos_z, sin_z], axis=0)
    z_imag = jnp.concatenate([-sin_z, cos_z], axis=0)
    y_real = jnp.stack([cos_y, sin_y], axis=1)
    y_imag = jnp.stack([-sin_y, cos_y], axis=1)
    y_matrix = jnp.stack([y_real, y_imag], axis=1).reshape(2 * size_y, 2 * size_y)
    cos_xs = cos_x.reshape(size_x, grid_count, slab_x)
    sin_xs = sin_x.reshape(size_x, grid_count, slab_x)
    x_real = jnp.stack([cos_xs, sin_xs], axis=2).reshape(size_x, 2 * size_x)
    x_imag = jnp.stack([-sin_xs, cos_xs], axis=2).reshape(size_x, 2 * size_x)

    pairs = []
    for a in range(block_bands):
        for b in range(a, block_bands):
            weight = occupation[a] * occupation[b] * (1.0 if a == b else 2.0)
            pairs.append((own[a], own[b], weight))
    pairs.sort(key=lambda pair: pair[0] is not pair[1])
    for distance in range(1, band_count // 2 + 1):
        there, there_occupied = others[distance]
        if 2 * distance < band_count:
            for a in range(block_bands):
                for b in range(block_bands):
                    pairs.append((own[a], there[b], 2.0 * occupation[a] * there_occupied[b]))
            continue
        for a in range(block_bands):
            for b in range(a + 1, block_bands):
                pairs.append((own[a], there[b], 2.0 * occupation[a] * there_occupied[b]))
        first = band_index < distance
        half = block_bands // 2
        for a in range(half):
            left = jnp.where(first, own[a], own[a + half])
            right = jnp.where(first, there[a], there[a + half])
            left_occupied = jnp.where(first, occupation[a], occupation[a + half])
            right_occupied = jnp.where(first, there_occupied[a], there_occupied[a + half])
            pairs.append((left, right, 2.0 * left_occupied * right_occupied))
        if block_bands % 2:
            last = block_bands - 1
            pairs.append((own[last], there[last], occupation[last] * there_occupied[last]))

    def density(pair):
        left, right, weight = pair
        return left * right * jnp.sqrt(weight)

    power = None
    for start in range(0, len(pairs), 2):
        first_density = density(pairs[start])
        if start + 1 < len(pairs):
            both = jnp.concatenate([first_density, density(pairs[start + 1])], axis=2)
            along_z = jnp.stack(
                [
                    jnp.einsum("yxz,zk->yxk", both, z_real, precision=HIGH),
                    jnp.einsum("yxz,zk->yxk", both, z_imag, precision=HIGH),
                ]
            )
        else:
            along_z = jnp.stack(
                [
                    jnp.einsum("yxz,zk->yxk", first_density, cos_z, precision=HIGH),
                    jnp.einsum("yxz,zk->yxk", first_density, -sin_z, precision=HIGH),
                ]
            )
        along_z = along_z.reshape(2 * size_y, slab_x, size_z)
        along_y = jnp.einsum("qp,pxk->qxk", y_matrix, along_z, precision=HIGH)
        received = lax.all_to_all(along_y, "grid", split_axis=0, concat_axis=0, tiled=True)
        received = received.reshape(grid_count, slab_y, 2, slab_x, size_z)
        lines = jnp.transpose(received, (1, 0, 2, 3, 4)).reshape(slab_y, 2 * size_x, size_z)
        real_part = jnp.einsum("np,rpk->rnk", x_real, lines, precision=HIGH)
        imag_part = jnp.einsum("np,rpk->rnk", x_imag, lines, precision=HIGH)
        pack_power = real_part * real_part + imag_part * imag_part
        power = pack_power if power is None else power + pack_power

    two_pi = 2.0 * math.pi
    kinds = widths.shape[0]
    one_hot = species[:, None] == jnp.arange(kinds, dtype=jnp.int32)[None, :]
    atom_width = jnp.sum(jnp.where(one_hot, widths[None, :], 0.0), axis=1)
    cell_x = jnp.arange(size_x, dtype=jnp.int32)
    cell_y = grid_index * slab_y + jnp.arange(slab_y, dtype=jnp.int32)
    cell_z = jnp.arange(size_z, dtype=jnp.int32)

    def factors(freq, length, fraction):
        wave = two_pi * freq / length
        turns = freq[:, None] * fraction[None, :]
        angles = two_pi * (turns - jnp.round(turns))
        damping = jnp.exp(-0.5 * (wave * wave)[:, None] * (atom_width * atom_width)[None, :])
        return damping * jnp.cos(angles), damping * jnp.sin(angles)

    stress = jnp.zeros((3, 3), jnp.float32)
    atom_terms = jnp.zeros(species.shape, jnp.float32)
    for which, nyquist_up in ((0, False), (1, True)):
        freq_x = folded(cell_x, size_x, nyquist_up)
        freq_y = folded(cell_y, size_y, nyquist_up)
        freq_z = folded(cell_z, size_z, nyquist_up)
        wave_x = (two_pi * freq_x / size_x)[None, :, None]
        wave_y = (two_pi * freq_y / size_y)[:, None, None]
        wave_z = (two_pi * freq_z / size_z)[None, None, :]
        wave_square = wave_x * wave_x + wave_y * wave_y + wave_z * wave_z
        nonzero = (wave_square > 0).astype(jnp.float32)
        denominator = wave_square + 1.0 - nonzero
        kept = masks[which] * (0.5 * scale * scale * 4.0 * math.pi) * nonzero / denominator
        weighted = power * kept
        along = weighted * 2.0 / denominator
        total = jnp.sum(weighted)
        waves = (wave_x, wave_y, wave_z)
        entries = {}
        for a in range(3):
            for b in range(a, 3):
                entries[a, b] = jnp.sum(along * waves[a] * waves[b])
        stress = stress + jnp.stack(
            [
                jnp.stack([entries[min(a, b), max(a, b)] for b in range(3)])
                for a in range(3)
            ]
        ) - total * jnp.eye(3, dtype=jnp.float32)
        xr, xi = factors(freq_x, size_x, positions[0])
        yr, yi = factors(freq_y, size_y, positions[1])
        zr, zi = factors(freq_z, size_z, positions[2])
        tr = jnp.einsum("rnk,kj->rnj", weighted, zr, precision=HIGH)
        ti = jnp.einsum("rnk,kj->rnj", weighted, zi, precision=HIGH)
        ur = jnp.sum(xr[None] * tr - xi[None] * ti, axis=1)
        ui = jnp.sum(xr[None] * ti + xi[None] * tr, axis=1)
        atom_terms = atom_terms + jnp.sum(yr * ur - yi * ui, axis=0)

    packed = jnp.concatenate([stress.reshape(-1), atom_terms]) / (block_bands * band_count)
    packed = lax.psum(packed, ("band", "grid"))
    return (packed[:9].reshape(3, 3), packed[9:])


def solution(mesh):
    return jax.shard_map(
        per_device,
        mesh=mesh,
        in_specs=(P("band", "grid", None, None), P("band"), P("grid"), P(), P(), P()),
        out_specs=(P(), P()),
        check_vma=False,
    )
```

time: 1360 us -> 514 us (0.38); the launches traced: 1330 us -> 504 us
  waiting for transfers between devices: 533 us -> 178 us
  matrix products: 391 us -> 77 us
  local copies, waits for them, and re-layouts: 237 us -> 30.9 us
  Pallas kernels: 0 us -> 74.1 us
  loops' own time: 54.2 us -> 0 us
  other arithmetic: 23.1 us -> 45.4 us
    all_to_all x6 -> x5, waiting for transfers between devices: 533 us -> 121 us  [per_device(): lax.all_to_all(along_y, 'grid', split_axis=0, concat_axis=0, tiled=True)]
    dot_general x82 -> x29, matrix products: 391 us -> 77 us  [the longest x5 19.7 us: per_device(): imag_part = jnp.einsum('np,rpk->rnk', x_imag, lines, precision=HIGH)]
    gather x1 -> x0, local copies, waits for them, and re-layouts: 90.5 us -> none  [per_device(): selected = jnp.take(flat_spectrum, g_list)]
    pallas_call x0 -> x1, Pallas kernels: none -> 74.1 us  [entry_masks(): pl.pallas_call(functools.partial(mask_kernel, chunks), grid=(3 * chunks,)...]
    ppermute x4, waiting for transfers between devices: 0.01 us -> 57.4 us  [shifted(): lax.ppermute(array, axis, [(i, (i + by) % peers) for i in range(peers)])]
    another operation x4 -> x0, loops' own time: 54.2 us -> none  [the longest x3 53.9 us: add_pairs(): return lax.fori_loop(0, block_bands, one_band, accumulated)]
    all_to_all x6 -> x0, local copies, waits for them, and re-layouts: 27.7 us -> none  [one_band(): lax.all_to_all(stacked, 'grid', split_axis=3, concat_axis=2, tiled=True)]
    another operation x6, local copies, waits for them, and re-layouts: 32.8 us -> 6.3 us  [the longest x4 4.87 us: per_device(): jnp.stack([jnp.einsum('yxz,zk->yxk', both, z_real, precision=HIGH), jnp.e...]
  transfers between devices with their start and end apart: 10 -> 11, of which waited for: 6 -> 5; matrix products, arithmetic and copies ran while one was open for 20% -> 16% of each run, Pallas kernels for 0% -> 15%
where the time goes in v1:
time: 514 us; the launch traced here: 504 us
  waiting for transfers between devices  178 us (35%)
  matrix products  77 us (15%)
  Pallas kernels  74.1 us (14%)
  other arithmetic  45.4 us (9%)
  starting transfers between devices  44.9 us (9%)
  blocking collectives  40 us (8%)
  local copies, waits for them, and re-layouts  30.9 us (6%)
  between operations  13.1 us (3%)
    all_to_all x5, waiting for transfers between devices, per_device(): lax.all_to_all(along_y, 'grid', split_axis=0, concat_axis=0, tiled=True)  121 us
    pallas_call x1, Pallas kernels, entry_masks(): pl.pallas_call(functools.partial(mask_kernel, chunks), grid=(3 * chunks,)...  74.1 us
    ppermute x4, waiting for transfers between devices, shifted(): lax.ppermute(array, axis, [(i, (i + by) % peers) for i in range(peers)])  57.4 us
    psum x1, blocking collectives, per_device(): packed = lax.psum(packed, ('band', 'grid'))  40 us
    all_to_all x5, starting transfers between devices, per_device(): lax.all_to_all(along_y, 'grid', split_axis=0, concat_axis=0, tiled=True)  37.7 us
    dot_general x5, matrix products, per_device(): imag_part = jnp.einsum('np,rpk->rnk', x_imag, lines, precision=HIGH)  19.7 us
    dot_general x5, matrix products, per_device(): real_part = jnp.einsum('np,rpk->rnk', x_real, lines, precision=HIGH)  16.9 us
    dot_general x5, local copies, waits for them, and re-layouts, per_device(): along_y = jnp.einsum('qp,pxk->qxk', y_matrix, along_z, precision=HIGH)  12.9 us
  transfers between devices with their start and end apart: 11, of which 5 were waited for; matrix products, arithmetic and copies ran while one was open for 16% of the time, Pallas kernels for 15%

profile of v1, /device:TPU:12, one launch (start us, length us, event | category | flops | bytes accessed | tf_op | source)
XLA Modules:
  0.0 504.0 jit_solution(14888282409461457832)
XLA Ops:
  0.7 1.6 collective-permute-start.2
  3.8 1.3 fusion.211
  13.9 57.4 %collective-permute-done.1 = f32[2]{0:T(128)S(1)} collective-permute-done((f32[2]{0:T(128)}, f32[2]{0:T(128)S(1)}, u32[]{:S(2)}, u32[]{:S(2)}) %collective-permute-start.1) | collective-permute-done | bytes 40 | tf_op jit(solution)/shard_map/ppermute | solution.py:16
  77.3 2.9 multiply_bitcast_fusion.1
  80.2 4.2 fusion.60
  87.8 1.6 fusion.6
  89.5 2.5 copy.135
  92.0 6.8 %all-to-all-start.1 = ((f32[256,16,128]{2,1,0:T(8,128)}), f32[256,16,128]{2,1,0:T(8,128)}, u32[]{:S(2)}, u32[]{:S(2)}) async-start(f32[256,16,128]{2,1,0:T(8,128)} %copy.135), calls=%async_computation.1 | async-start | bytes 4194304 | tf_op jit(solution)/shard_map/all_to_all | solution.py:179
  98.8 2.7 fusion.19
  104.0 1.6 fusion.8
  105.6 2.6 copy.132
  108.2 34.9 %all-to-all-done.1 = f32[256,16,128]{2,1,0:T(8,128)} async-done(((f32[256,16,128]{2,1,0:T(8,128)}), f32[256,16,128]{2,1,0:T(8,128)}, u32[]{:S(2)}, u32[]{:S(2)}) %all-to-all-start.1) | async-done | bytes 2097184 | tf_op jit(solution)/shard_map/all_to_all | solution.py:179
  143.1 7.6 %all-to-all-start = ((f32[256,16,128]{2,1,0:T(8,128)}), f32[256,16,128]{2,1,0:T(8,128)}, u32[]{:S(2)}, u32[]{:S(2)}) async-start(f32[256,16,128]{2,1,0:T(8,128)} %copy.132), calls=%async_computation | async-start | bytes 4194304 | tf_op jit(solution)/shard_map/all_to_all | solution.py:179
  150.7 1.5 collective-permute-start.4
  152.2 2.6 collective-permute-start.5
  157.3 1.8 fusion.23
  161.6 1.6 fusion.4
  163.2 2.6 copy.138
  165.9 32.3 %all-to-all-done = f32[256,16,128]{2,1,0:T(8,128)} async-done(((f32[256,16,128]{2,1,0:T(8,128)}), f32[256,16,128]{2,1,0:T(8,128)}, u32[]{:S(2)}, u32[]{:S(2)}) %all-to-all-start) | async-done | bytes 2097184 | tf_op jit(solution)/shard_map/all_to_all | solution.py:179
  198.2 8.5 %all-to-all-start.2 = ((f32[256,16,128]{2,1,0:T(8,128)}), f32[256,16,128]{2,1,0:T(8,128)}, u32[]{:S(2)}, u32[]{:S(2)}) async-start(f32[256,16,128]{2,1,0:T(8,128)} %copy.138), calls=%async_computation.2 | async-start | bytes 4194304 | tf_op jit(solution)/shard_map/all_to_all | solution.py:179
  210.8 3.2 cosine_multiply_fusion.1
  215.2 1.7 add_select_fusion.2
  216.9 1.7 add_select_fusion
  218.6 1.8 fusion.25
  222.9 1.6 fusion.2
  224.5 2.6 copy.141
  227.1 23.3 %all-to-all-done.2 = f32[256,16,128]{2,1,0:T(8,128)} async-done(((f32[256,16,128]{2,1,0:T(8,128)}), f32[256,16,128]{2,1,0:T(8,128)}, u32[]{:S(2)}, u32[]{:S(2)}) %all-to-all-start.2) | async-done | bytes 2097184 | tf_op jit(solution)/shard_map/all_to_all | solution.py:179
  250.4 7.3 %all-to-all-start.3 = ((f32[256,16,128]{2,1,0:T(8,128)}), f32[256,16,128]{2,1,0:T(8,128)S(1)}, u32[]{:S(2)}, u32[]{:S(2)}) async-start(f32[256,16,128]{2,1,0:T(8,128)} %copy.141), calls=%async_computation.3 | async-start | bytes 4194304 | tf_op jit(solution)/shard_map/all_to_all | solution.py:179
  257.7 1.8 pad_add_fusion
  259.5 1.9 reshape.738.row_ref
  261.4 1.7 pad_add_fusion.1
  263.1 1.9 reshape.739.col_ref
  268.1 1.6 fusion
  269.8 2.6 copy.144
  272.3 30.5 %all-to-all-done.3 = f32[256,16,128]{2,1,0:T(8,128)S(1)} async-done(((f32[256,16,128]{2,1,0:T(8,128)}), f32[256,16,128]{2,1,0:T(8,128)S(1)}, u32[]{:S(2)}, u32[]{:S(2)}) %all-to-all-start.3) | async-done | bytes 2097184 | tf_op jit(solution)/shard_map/all_to_all | solution.py:179
  302.8 1.4 copy-done.6
  304.2 7.5 %all-to-all-start.4 = ((f32[256,16,128]{2,1,0:T(8,128)}), f32[256,16,128]{2,1,0:T(8,128)}, u32[]{:S(2)}, u32[]{:S(2)}) async-start(f32[256,16,128]{2,1,0:T(8,128)} %copy.144), calls=%async_computation.4 | async-start | bytes 4194304 | tf_op jit(solution)/shard_map/all_to_all | solution.py:179
  311.7 74.1 %entry_masks.1 = f32[2,2048,128]{2,1,0:T(8,128)} custom-call(s32[96,1,512]{2,1,0:T(1,128)} %reshape.738.row_ref, s32[96,1,512]{2,1,0:T(1,128)} %reshape.739.col_ref), custom_call_target="tpu_custom_call" | custom-call | flops 51539607552 | bytes 2097152 | tf_op jit(solution)/shard_map/entry_masks/pallas_call | solution.py:57
  385.8 1.7 slice_multiply_fusion.1
  387.9 1.4 copy.146
  389.2 4.4 fusion.32
  393.6 4.4 fusion.34
  398.1 4.5 fusion.30
  402.6 2.9 fusion.28
  405.5 3.5 fusion.26
  409.0 3.5 fusion.38
  412.6 3.7 fusion.37
  416.3 3.5 fusion.40
  419.9 1.9 fusion.42
  421.9 4.3 fusion.204
  426.1 1.7 multiply_reduce_fusion.4
  427.8 2.0 maximum_bitcast_fusion.27
  429.8 2.0 maximum_bitcast_fusion.28
  431.7 1.9 maximum_bitcast_fusion.29
  433.7 4.7 fusion.67
  438.5 5.0 fusion.71
  443.5 1.7 multiply_reduce_fusion.10
  445.2 1.9 maximum_bitcast_fusion.24
  447.1 1.9 maximum_bitcast_fusion.25
  449.0 1.9 maximum_bitcast_fusion.26
  450.9 1.3 fusion.165
  452.3 5.6 %subtract_reduce_fusion.1 = (f32[16,512]{1,0:T(8,128)S(1)}, f32[16,512]{1,0:T(8,128)S(1)}) fusion(f32[16,128,512]{2,1,0:T(8,128)} %fusion.71, f32[128,512]{1,0:T(8,128)S(1)} %copy-done.15, f32[128,512]{1,0:T(8,128)S(1)} %copy-done.14, f32[16,128,128]{1,2,0:T(8,128)S(1)} %get-tuple-element.21, f32[512]{0:T(512)S(1)} %bitcast.282, f32[128]{0:T(128)S(1)} %copy-done.30, ...), kind=kOutput, calls=%fused_computation.3 | convolution fusion | flops 814071808 | bytes 5837824 | tf_op jit(solution)/shard_map/rnk,kj->rnj/dot_general | solution.py:233
  458.0 3.9 subtract_reduce_fusion
  462.4 40.0 %psum.7 = f32[521]{0:T(1024)S(1)} all-reduce(f32[521]{0:T(1024)S(1)} %maximum_multiply_fusion), channel_id=1, replica_groups=mesh['band'=4,'grid'=8] {'band','grid'}, use_global_device_ids=true, to_apply=%region_21.22 | all-reduce | flops 521 | bytes 4168 | tf_op jit(solution)/shard_map/psum | solution.py:239
  (160 shorter events, 28.9 us)
Async XLA Ops:
  0.6 76.7 %collective-permute-start = (f32[2,128,16,128]{3,1,2,0:T(8,128)}, f32[2,128,16,128]{3,1,2,0:T(8,128)}, u32[]{:S(2)}, u32[]{:S(2)}) collective-permute-start(f32[2,128,16,128]{3,1,2,0:T(8,128)} %bitcast.261), channel_id=1, source_target_pairs={{0,8},{8,16},{16,24},{24,0},{1,9},{9,17},{17,25},{25,1},{2,10},{10... | collective-permute-start | bytes 6291464 | tf_op jit(solution)/shard_map/ppermute | solution.py:16
  0.7 79.5 %collective-permute-start.2 = (f32[2,128,16,128]{3,1,2,0:T(8,128)}, f32[2,128,16,128]{3,1,2,0:T(8,128)}, u32[]{:S(2)}, u32[]{:S(2)}) collective-permute-start(f32[2,128,16,128]{3,1,2,0:T(8,128)} %bitcast.262), channel_id=1, source_target_pairs={{0,16},{8,24},{16,0},{24,8},{1,17},{9,25},{17,1},{25,9},{2,18},{10... | collective-permute-start | bytes 6291464 | tf_op jit(solution)/shard_map/ppermute | solution.py:16
  2.3 72.2 %collective-permute-start.3 = (f32[2]{0:T(128)}, f32[2]{0:T(128)S(1)}, u32[]{:S(2)}, u32[]{:S(2)}) collective-permute-start(f32[2]{0:T(128)} %param.7), channel_id=1, source_target_pairs={{0,16},{8,24},{16,0},{24,8},{1,17},{9,25},{17,1},{25,9},{2,18},{10... | collective-permute-start | bytes 32 | tf_op jit(solution)/shard_map/ppermute | solution.py:16
  2.8 68.5 %collective-permute-start.1 = (f32[2]{0:T(128)}, f32[2]{0:T(128)S(1)}, u32[]{:S(2)}, u32[]{:S(2)}) collective-permute-start(f32[2]{0:T(128)} %param.7), channel_id=1, source_target_pairs={{0,8},{8,16},{16,24},{24,0},{1,9},{9,17},{17,25},{25,1},{2,10},{10... | collective-permute-start | bytes 32 | tf_op jit(solution)/shard_map/ppermute | solution.py:16
  77.3 2.9 copy-start.4
  80.2 4.2 copy-start.8
  92.0 51.1 %all-to-all-start.1 = ((f32[256,16,128]{2,1,0:T(8,128)}), f32[256,16,128]{2,1,0:T(8,128)}, u32[]{:S(2)}, u32[]{:S(2)}) async-start(f32[256,16,128]{2,1,0:T(8,128)} %copy.135), calls=%async_computation.1 | async-start | bytes 4194304 | tf_op jit(solution)/shard_map/all_to_all | solution.py:179
  98.8 2.7 copy-start.1
  98.8 2.7 copy-start.2
  108.2 48.4 %copy-start.37 = (s32[512]{0:T(512)S(1)}, s32[512]{0:T(512)}, u32[]{:S(2)}) copy-start(s32[512]{0:T(512)} %param.10) | copy-start | bytes 6148
  143.1 55.1 %all-to-all-start = ((f32[256,16,128]{2,1,0:T(8,128)}), f32[256,16,128]{2,1,0:T(8,128)}, u32[]{:S(2)}, u32[]{:S(2)}) async-start(f32[256,16,128]{2,1,0:T(8,128)} %copy.132), calls=%async_computation | async-start | bytes 4194304 | tf_op jit(solution)/shard_map/all_to_all | solution.py:179
  150.7 64.6 %collective-permute-start.4 = (s32[16384]{0:T(1024)}, s32[16384]{0:T(1024)}, u32[]{:S(2)}, u32[]{:S(2)}) collective-permute-start(s32[16384]{0:T(1024)} %param.8), channel_id=1, source_target_pairs={{0,7},{1,6},{2,5},{3,4},{4,3},{5,2},{6,1},{7,0},{8,15},{9,14},{10,... | collective-permute-start | bytes 196616 | tf_op jit(solution)/shard_map/ppermute | solution.py:94
  152.2 64.8 %collective-permute-start.5 = (s32[16384]{0:T(1024)}, s32[16384]{0:T(1024)}, u32[]{:S(2)}, u32[]{:S(2)}) collective-permute-start(s32[16384]{0:T(1024)} %param.8), channel_id=1, source_target_pairs={{0,0},{1,7},{2,6},{3,5},{4,4},{5,3},{6,2},{7,1},{8,8},{9,15},{10,1... | collective-permute-start | bytes 196616 | tf_op jit(solution)/shard_map/ppermute | solution.py:97
  154.8 53.6 %copy-start.25 = (f32[128]{0:T(128)}, f32[128]{0:T(128)S(1)}, u32[]{:S(2)}) copy-start(f32[128]{0:T(128)S(1)} %get-tuple-element.75) | copy-start | bytes 1540
  154.8 54.3 %copy-start.23 = (f32[128]{0:T(128)}, f32[128]{0:T(128)S(1)}, u32[]{:S(2)}) copy-start(f32[128]{0:T(128)S(1)} %get-tuple-element.76) | copy-start | bytes 1540
  165.8 42.6 %copy-start.45 = (f32[16]{0:T(128)S(1)}, f32[16]{0:T(128)}, u32[]{:S(2)}) copy-start(f32[16]{0:T(128)} %get-tuple-element.70) | copy-start | bytes 196
  165.8 43.3 %copy-start.44 = (f32[16]{0:T(128)S(1)}, f32[16]{0:T(128)}, u32[]{:S(2)}) copy-start(f32[16]{0:T(128)} %get-tuple-element.69) | copy-start | bytes 196
  165.8 43.3 %copy-start.22 = (f32[3,512]{1,0:T(4,128)S(1)}, f32[3,512]{1,0:T(4,128)}, u32[]{:S(2)}) copy-start(f32[3,512]{1,0:T(4,128)} %param.9) | copy-start | bytes 18436
  165.8 45.0 %copy-start.27 = (f32[128]{0:T(128)S(1)}, f32[128]{0:T(128)}, u32[]{:S(2)}) copy-start(f32[128]{0:T(128)} %get-tuple-element.78) | copy-start | bytes 1540
  165.8 44.9 %copy-start.29 = (f32[128]{0:T(128)S(1)}, f32[128]{0:T(128)}, u32[]{:S(2)}) copy-start(f32[128]{0:T(128)} %get-tuple-element.77) | copy-start | bytes 1540
  165.8 48.1 %copy-start.16 = (s32[16384]{0:T(1024)S(1)}, s32[16384]{0:T(1024)}, u32[]{:S(2)}) copy-start(s32[16384]{0:T(1024)} %param.8) | copy-start | bytes 196612
  165.9 52.7 %copy-start = (f32[128,16,128]{2,0,1:T(8,128)S(1)}, f32[128,16,128]{2,0,1:T(8,128)}, u32[]{:S(2)}) copy-start(f32[128,16,128]{2,0,1:T(8,128)} %get-tuple-element.25) | copy-start | bytes 3145732
  198.2 52.3 %all-to-all-start.2 = ((f32[256,16,128]{2,1,0:T(8,128)}), f32[256,16,128]{2,1,0:T(8,128)}, u32[]{:S(2)}, u32[]{:S(2)}) async-start(f32[256,16,128]{2,1,0:T(8,128)} %copy.138), calls=%async_computation.2 | async-start | bytes 4194304 | tf_op jit(solution)/shard_map/all_to_all | solution.py:179
  207.2 11.4 %copy-start.31 = (f32[128]{0:T(128)}, f32[128]{0:T(128)S(1)}, u32[]{:S(2)}) copy-start(f32[128]{0:T(128)S(1)} %get-tuple-element.79) | copy-start | bytes 1540
  207.2 11.4 %copy-start.33 = (f32[128]{0:T(128)}, f32[128]{0:T(128)S(1)}, u32[]{:S(2)}) copy-start(f32[128]{0:T(128)S(1)} %get-tuple-element.80) | copy-start | bytes 1540
  227.1 34.3 %copy-start.10 = (s32[16384]{0:T(1024)S(1)}, s32[16384]{0:T(1024)}, u32[]{:S(2)}) copy-start(s32[16384]{0:T(1024)} %get-tuple-element.37) | copy-start | bytes 196612
  227.1 34.3 %copy-start.11 = (s32[16384]{0:T(1024)S(1)}, s32[16384]{0:T(1024)}, u32[]{:S(2)}) copy-start(s32[16384]{0:T(1024)} %get-tuple-element.39) | copy-start | bytes 196612
  227.1 37.9 %copy-start.3 = (f32[128,16,128]{2,0,1:T(8,128)S(1)}, f32[128,16,128]{2,0,1:T(8,128)}, u32[]{:S(2)}) copy-start(f32[128,16,128]{2,0,1:T(8,128)} %get-tuple-element.24) | copy-start | bytes 3145732
  250.4 52.4 %all-to-all-start.3 = ((f32[256,16,128]{2,1,0:T(8,128)}), f32[256,16,128]{2,1,0:T(8,128)S(1)}, u32[]{:S(2)}, u32[]{:S(2)}) async-start(f32[256,16,128]{2,1,0:T(8,128)} %copy.141), calls=%async_computation.3 | async-start | bytes 4194304 | tf_op jit(solution)/shard_map/all_to_all | solution.py:179
  302.8 1.4 copy-start.6
  304.2 101.3 %all-to-all-start.4 = ((f32[256,16,128]{2,1,0:T(8,128)}), f32[256,16,128]{2,1,0:T(8,128)}, u32[]{:S(2)}, u32[]{:S(2)}) async-start(f32[256,16,128]{2,1,0:T(8,128)} %copy.144), calls=%async_computation.4 | async-start | bytes 4194304 | tf_op jit(solution)/shard_map/all_to_all | solution.py:179
  387.5 1.7 copy-start.18
  387.5 1.7 copy-start.19
  398.1 4.5 copy-start.7
  405.5 3.5 copy-start.17
  405.5 3.5 copy-start.49
  409.0 3.5 copy-start.48
  412.6 3.7 copy-start.47
  416.3 3.6 copy-start.46
  419.8 1.9 copy-start.9
  419.9 1.9 copy-start.20
  419.9 1.9 copy-start.24
  419.9 1.9 copy-start.26
  421.8 4.3 copy-start.35
  421.8 4.3 copy-start.39
  421.8 11.8 %copy-start.28 = (f32[128]{0:T(128)S(1)}, f32[128]{0:T(128)}, u32[]{:S(2)}) copy-start(f32[128]{0:T(128)} %get-tuple-element.78) | copy-start | bytes 1540
  421.9 11.8 %copy-start.32 = (f32[128]{0:T(128)S(1)}, f32[128]{0:T(128)}, u32[]{:S(2)}) copy-start(f32[128]{0:T(128)} %copy-done.31) | copy-start | bytes 1540
  433.7 4.7 copy-start.30
  433.7 4.7 copy-start.34
  438.4 5.1 %copy-start.36 = (f32[128]{0:T(128)S(1)}, f32[128]{0:T(128)}, u32[]{:S(2)}) copy-start(f32[128]{0:T(128)} %broadcast_multiply_fusion.7) | copy-start | bytes 1540
  438.4 5.1 %copy-start.38 = (f32[16]{0:T(128)S(1)}, f32[16]{0:T(128)}, u32[]{:S(2)}) copy-start(f32[16]{0:T(128)} %get-tuple-element.68) | copy-start | bytes 196
  438.4 13.8 %copy-start.14 = (f32[128,512]{1,0:T(8,128)S(1)}, f32[128,512]{1,0:T(8,128)}, u32[]{:S(2)}) copy-start(f32[128,512]{1,0:T(8,128)} %get-tuple-element.48) | copy-start | bytes 786436
  438.4 13.8 %copy-start.15 = (f32[128,512]{1,0:T(8,128)S(1)}, f32[128,512]{1,0:T(8,128)}, u32[]{:S(2)}) copy-start(f32[128,512]{1,0:T(8,128)} %get-tuple-element.49) | copy-start | bytes 786436
  452.2 5.7 %copy-start.5 = (f32[16,128,512]{2,1,0:T(8,128)S(1)}, f32[16,128,512]{2,1,0:T(8,128)}, u32[]{:S(2)}) copy-start(f32[16,128,512]{2,1,0:T(8,128)} %fusion.67) | copy-start | bytes 12582916
  452.2 5.7 %copy-start.12 = (f32[128,512]{1,0:T(8,128)S(1)}, f32[128,512]{1,0:T(8,128)}, u32[]{:S(2)}) copy-start(f32[128,512]{1,0:T(8,128)} %get-tuple-element.52) | copy-start | bytes 786436
  452.2 5.7 %copy-start.13 = (f32[128,512]{1,0:T(8,128)S(1)}, f32[128,512]{1,0:T(8,128)}, u32[]{:S(2)}) copy-start(f32[128,512]{1,0:T(8,128)} %get-tuple-element.53) | copy-start | bytes 786436
  457.9 4.0 copy-start.21
  457.9 4.0 copy-start.40
  457.9 4.0 copy-start.41
  458.0 4.0 copy-start.42
  458.0 4.0 copy-start.43
